TPU v7x, 32 devices: a whole 2x2x4 slice. The times are simulated.
32 devices in a mesh: groups: 2 (over x), expert: 16 (over z, y, core), beam: 1.
Axes of the slice: x: 2, y: 2, z: 4, core: 2. Of those that a mesh axis runs over, the one named last changes fastest.
Arguments:
- queries: bfloat16 [128, 2048], P(('groups', 'expert', 'beam')), parts along dimension 0, may hold values from -64 to 64
- new_keys: bfloat16 [128, 2048], P(('groups', 'expert', 'beam')), parts along dimension 0, may hold values from -4 to 4
- new_values: bfloat16 [128, 2048], P(('groups', 'expert', 'beam')), parts along dimension 0, may hold values from -4 to 4
- resid: bfloat16 [128, 2048], P(('groups', 'expert', 'beam')), parts along dimension 0, may hold values from -5 to 5
- key_cache: bfloat16 [128, 128, 2048], P(('groups', 'expert', 'beam')), parts along dimension 0, may hold values from -4 to 4
- value_cache: bfloat16 [128, 128, 2048], P(('groups', 'expert', 'beam')), parts along dimension 0, may hold values from -4 to 4
- parent: int32 [128], P('groups'), parts along dimension 0, may hold values from 0 to 63, as said below
- route_ids: int32 [128, 6], P('groups'), parts along dimension 0, may hold values from 0 to 15, all different within a row; in each aligned block of 4 rows (0 to 3, 4 to 7, ...) at most 2 rows name the same one
- route_weights: float32 [128, 6], P('groups'), parts along dimension 0, may hold values from 0.05 to 0.35
- norm_gain: float32 [2048], replicated, may hold values from 0.1 to 1.9
- w_gate: bfloat16 [16, 2048, 1408], P('expert', None, 'beam'), may hold values from -0.125 to 0.125
- w_up: bfloat16 [16, 2048, 1408], P('expert', None, 'beam'), may hold values from -0.125 to 0.125
- w_down: bfloat16 [16, 1408, 2048], P('expert', 'beam'), may hold values from -0.15625 to 0.15625
Outputs:
- layer_out: bfloat16 [128, 2048], P(('groups', 'expert', 'beam')), parts along dimension 0
There are 2 independent parts, one for each index of `groups`. A program takes and returns all parts, laid end to end along the dimension named above; an argument that names none is the same for every part. Nothing has to cross between parts.
Inputs may be any that keep to these rules, and one draw needn't show every extreme that they name: `parent`: a permutation of 0 to 63. `route_ids`: the 6 experts of a slot differ; among the 4 slots of one device no expert is named by more than 2 slots, and this is reached.
All inputs are finite; a program needn't handle non-finite values.
Results may differ from a plain program's by a relative error of at most 0.0065.
Values may be sent and summed in bfloat16 or wider, within the bound.
A program may use at most 64 MiB of HBM per device.

v0:
```python
import math

import jax
import jax.numpy as jnp
from jax import lax
from jax.sharding import PartitionSpec as P

HEAD_DIM = 128


def attend(query_rows, new_key_rows, new_value_rows, key_cache, value_cache):
    slots, positions, width = key_cache.shape
    head_size = HEAD_DIM
    head_count = width // head_size
    scale = 1.0 / math.sqrt(head_size)
    query_heads = query_rows.reshape(slots, head_count, head_size)
    key_heads = key_cache.reshape(slots, positions, head_count, head_size)
    value_heads = value_cache.reshape(slots, positions, head_count, head_size)
    new_key_heads = new_key_rows.reshape(slots, head_count, head_size).astype(jnp.float32)
    new_value_heads = new_value_rows.reshape(slots, head_count, head_size).astype(jnp.float32)
    scores = (
        jnp.einsum("bhd,bthd->bht", query_heads, key_heads, preferred_element_type=jnp.float32)
        * scale
    )
    self_score = jnp.sum(query_heads.astype(jnp.float32) * new_key_heads, axis=-1) * scale
    peak = jnp.maximum(jnp.max(scores, axis=-1), self_score)
    expo = jnp.exp(scores - peak[:, :, None])
    self_expo = jnp.exp(self_score - peak)
    denominator = jnp.sum(expo, axis=-1) + self_expo
    probs_bf = expo.astype(jnp.bfloat16)
    self_bf = self_expo.astype(jnp.bfloat16).astype(jnp.float32)
    mixed = jnp.einsum("bht,bthd->bhd", probs_bf, value_heads, preferred_element_type=jnp.float32)
    mixed = mixed + self_bf[:, :, None] * new_value_heads
    return (mixed / denominator[:, :, None]).reshape(slots, width).astype(jnp.bfloat16)


def expert_rows_out(flat, w_gate, w_up, w_down):
    gate_act = jnp.dot(flat, w_gate[0], preferred_element_type=jnp.float32)
    up_act = jnp.dot(flat, w_up[0], preferred_element_type=jnp.float32)
    inner = (jax.nn.silu(gate_act) * up_act).astype(jnp.bfloat16)
    return jnp.dot(inner, w_down[0], preferred_element_type=jnp.float32)


def body(
    queries,
    new_keys,
    new_values,
    resid,
    key_cache,
    value_cache,
    parent,
    route_ids,
    route_weights,
    norm_gain,
    w_gate,
    w_up,
    w_down,
):
    rows_here = queries.shape[0]
    position = lax.axis_index(("expert", "beam"))
    gathered = (
        lax.all_gather(queries, ("expert", "beam"), axis=0, tiled=True),
        lax.all_gather(new_keys, ("expert", "beam"), axis=0, tiled=True),
        lax.all_gather(new_values, ("expert", "beam"), axis=0, tiled=True),
        lax.all_gather(resid, ("expert", "beam"), axis=0, tiled=True),
    )
    slot_ids = position * rows_here + jnp.arange(rows_here, dtype=jnp.int32)
    picker = (parent[None, :] == slot_ids[:, None]).astype(jnp.bfloat16)
    picked = [
        jnp.dot(picker, source_rows, preferred_element_type=jnp.float32).astype(jnp.bfloat16)
        for source_rows in gathered
    ]
    attended = attend(picked[0], picked[1], picked[2], key_cache, value_cache)
    hidden_state = picked[3].astype(jnp.float32) + attended.astype(jnp.float32)
    normed = (
        hidden_state
        * lax.rsqrt(jnp.mean(hidden_state * hidden_state, axis=-1, keepdims=True) + 1e-06)
        * norm_gain
    ).astype(jnp.bfloat16)
    chosen = route_ids.shape[1]
    experts = lax.axis_size("expert")
    own_ids = lax.dynamic_slice_in_dim(route_ids, position * rows_here, rows_here, 0)
    own_weights = lax.dynamic_slice_in_dim(route_weights, position * rows_here, rows_here, 0)
    expert_ids = jnp.arange(experts, dtype=jnp.int32)
    matches = own_ids[:, :, None] == expert_ids[None, None, :]
    named = jnp.any(matches, axis=1).astype(jnp.int32)
    coef_own = jnp.sum(own_weights[:, :, None] * matches, axis=1)
    ranks = jnp.cumsum(named, axis=0) - named
    capacity = max(2, (rows_here * chosen + experts - 1) // experts)
    slot_numbers = jnp.arange(capacity, dtype=jnp.int32)
    placed = (named.T[:, None, :] == 1) & (ranks.T[:, None, :] == slot_numbers[None, :, None])
    outgoing = jnp.einsum(
        "esb,bd->esd", placed.astype(jnp.bfloat16), normed, preferred_element_type=jnp.float32
    ).astype(jnp.bfloat16)
    both = lax.all_gather(
        lax.all_to_all(outgoing, "expert", split_axis=0, concat_axis=0, tiled=True),
        "beam",
        axis=0,
        tiled=True,
    )
    sources, items, depth = both.shape
    partial_out = expert_rows_out(both.reshape(sources * items, depth), w_gate, w_up, w_down)
    summed = lax.psum_scatter(
        partial_out.reshape(sources, items, depth), "beam", scatter_dimension=0, tiled=True
    )
    returned = lax.all_to_all(summed, "expert", split_axis=0, concat_axis=0, tiled=True)
    combine_weights = placed.astype(jnp.float32) * coef_own.T[:, None, :]
    moe_sum = jnp.einsum("esb,esd->bd", combine_weights, returned, precision=lax.Precision.HIGHEST)
    return (hidden_state + moe_sum).astype(jnp.bfloat16)


def solution(mesh):
    return jax.shard_map(
        body,
        mesh=mesh,
        in_specs=(
            P(("groups", "expert", "beam"), None),
            P(("groups", "expert", "beam"), None),
            P(("groups", "expert", "beam"), None),
            P(("groups", "expert", "beam"), None),
            P(("groups", "expert", "beam"), None, None),
            P(("groups", "expert", "beam"), None, None),
            P("groups"),
            P("groups", None),
            P("groups", None),
            P(),
            P("expert", None, "beam"),
            P("expert", None, "beam"),
            P("expert", "beam", None),
        ),
        out_specs=P(("groups", "expert", "beam"), None),
        check_vma=False,
    )
```

profile of v0, /device:TPU:0, one launch (start us, length us, event | category | flops | bytes accessed | tf_op | source)
XLA Modules:
  0.0 127.4 jit_solution(8733624560338123352)
XLA Ops:
  0.0 0.0 copy-start
  0.0 0.0 copy-start.4
  0.0 0.0 copy-start.1
  0.0 0.0 copy-start.2
  0.0 24.2 %all-gather.1 = bf16[16,4,2048]{2,1,0:T(4,128)(2,1)S(1)} all-gather(bf16[1,4,2048]{2,1,0:T(4,128)(2,1)} %bitcast.84), channel_id=1, replica_groups=mesh['groups'=2,'expert'=16,'beam'=1] {'expert','beam'}, dimensions={0}, use_global_device_ids=true | all-gather | bytes 278528 | tf_op jit(solution)/shard_map/all_gather | solution.py:62
  24.2 0.1 reshape.75
  24.3 0.9 convolution_convert_fusion.3
  25.2 0.0 copy-start.5
  25.2 0.0 copy-start.3
  25.2 4.0 %copy.35 = bf16[4,128,2048]{1,2,0:T(8,128)(2,1)} copy(bf16[4,128,2048]{2,1,0:T(8,128)(2,1)} %param.17) | data formatting | bytes 4194304 | tf_op jit(solution)/shard_map/reshape | solution.py:17
  29.2 18.4 %all-gather.2 = bf16[16,4,2048]{2,1,0:T(4,128)(2,1)S(1)} all-gather(bf16[1,4,2048]{2,1,0:T(4,128)(2,1)} %bitcast.85), channel_id=1, replica_groups=mesh['groups'=2,'expert'=16,'beam'=1] {'expert','beam'}, dimensions={0}, use_global_device_ids=true | all-gather | bytes 278528 | tf_op jit(solution)/shard_map/all_gather | solution.py:63
  47.6 0.1 reshape.77
  47.7 0.0 copy-done.4
  47.7 0.2 fusion.21
  47.9 2.2 %fusion.62 = f32[4,16,1,128]{3,2,1,0:T(1,128)S(1)} fusion(bf16[4,16,128,1]{2,3,1,0:T(2,128)(2,1)S(1)} %reshape.88, bf16[4,128,16,128]{1,3,2,0:T(8,128)(2,1)} %bitcast.79), kind=kOutput, calls=%fused_computation.80 | convolution fusion | flops 2097152 | bytes 2146304 | tf_op jit(solution)/shard_map/bhd,bthd->bht/dot_general | solution.py:22
  50.1 0.1 fusion.28
  50.2 0.2 fusion.32
  50.4 0.0 copy-done.1
  50.4 19.4 %all-gather.3 = bf16[16,4,2048]{2,1,0:T(4,128)(2,1)S(1)} all-gather(bf16[1,4,2048]{2,1,0:T(4,128)(2,1)S(1)} %bitcast.86), channel_id=1, replica_groups=mesh['groups'=2,'expert'=16,'beam'=1] {'expert','beam'}, dimensions={0}, use_global_device_ids=true | all-gather | bytes 278528 | tf_op jit(solution)/shard_map/all_gather | solution.py:64
  69.9 0.1 reshape.79
  69.9 0.2 fusion.22
  70.2 0.0 copy-done.2
  70.2 18.2 %all-gather = bf16[16,4,2048]{2,1,0:T(4,128)(2,1)S(1)} all-gather(bf16[1,4,2048]{2,1,0:T(4,128)(2,1)S(1)} %bitcast.87), channel_id=1, replica_groups=mesh['groups'=2,'expert'=16,'beam'=1] {'expert','beam'}, dimensions={0}, use_global_device_ids=true | all-gather | bytes 278528 | tf_op jit(solution)/shard_map/all_gather | solution.py:65
  88.3 0.1 reshape.73
  88.4 0.0 copy-done
  88.4 0.6 fusion.18
  89.1 0.1 convert_bitcast_fusion
  89.2 0.3 multiply_reduce_fusion
  89.5 0.0 copy-done.5
  89.5 0.1 constant_dynamic-slice_fusion.1
  89.6 0.1 fusion.37
  89.7 0.0 copy-done.3
  89.7 0.2 convolution_convert_fusion
  90.0 0.1 copy.25
  90.1 10.7 %all_to_all.10 = bf16[16,2,2048]{2,1,0:T(2,128)(2,1)S(1)} all-to-all(bf16[16,2,2048]{2,1,0:T(2,128)(2,1)S(1)} %copy.25), channel_id=1, replica_groups=mesh['groups'=2,'expert'=16,'beam'=1] {'expert'}, dimensions={0} | all-to-all | bytes 262144 | tf_op jit(solution)/shard_map/all_to_all | solution.py:96
  100.8 0.1 reshape.68
  100.9 3.7 %fusion.4 = f32[32,1408]{1,0:T(8,128)S(1)} fusion(bf16[32,2048]{1,0:T(8,128)(2,1)S(1)} %reshape.68, bf16[1,2048,1408]{2,1,0:T(8,128)(2,1)} %param.23), kind=kOutput, calls=%fused_computation.4 | convolution fusion | flops 184549376 | bytes 6078464 | tf_op jit(solution)/shard_map/dot_general | solution.py:38
  104.6 0.0 copy-start.6
  104.6 3.7 %fusion.9 = bf16[32,1408]{1,0:T(8,128)(2,1)S(1)} fusion(bf16[32,2048]{1,0:T(8,128)(2,1)S(1)} %reshape.68, bf16[1,2048,1408]{2,1,0:T(8,128)(2,1)} %param.24, f32[32,1408]{1,0:T(8,128)S(1)} %fusion.4), kind=kOutput, calls=%fused_computation.7 | convolution fusion | flops 184819712 | bytes 6168576 | tf_op jit(solution)/shard_map/dot_general | solution.py:39
  108.3 3.7 %fusion = f32[16,2,2048]{2,0,1:T(8,128)S(1)} fusion(bf16[1,1408,2048]{2,1,0:T(8,128)(2,1)} %param.25, bf16[16,2,1408]{2,1,0:T(2,128)(2,1)S(1)} %dot_general.44), kind=kOutput, calls=%fused_computation | convolution fusion | flops 184549376 | bytes 6119424 | tf_op jit(solution)/shard_map/dot_general | solution.py:41
  112.0 0.9 copy.27
  112.9 3.5 %all-to-all-start.1 = ((f32[16,2,2048]{2,1,0:T(2,128)}), f32[16,2,2048]{2,1,0:T(2,128)S(1)}, u32[]{:S(2)}, u32[]{:S(2)}) async-start(f32[16,2,2048]{2,1,0:T(2,128)} %copy.27), calls=%async_computation.1 | async-start | bytes 524288 | tf_op jit(solution)/shard_map/all_to_all | solution.py:106
  116.5 0.0 copy-done.6
  116.5 0.1 constant_dynamic-slice_fusion
  116.6 0.1 select_reduce_fusion
  116.6 9.8 %all-to-all-done.1 = f32[16,2,2048]{2,1,0:T(2,128)S(1)} async-done(((f32[16,2,2048]{2,1,0:T(2,128)}), f32[16,2,2048]{2,1,0:T(2,128)S(1)}, u32[]{:S(2)}, u32[]{:S(2)}) %all-to-all-start.1) | async-done | bytes 262176 | tf_op jit(solution)/shard_map/all_to_all | solution.py:106
  126.5 1.0 fusion.13
  (9 shorter events, 0.2 us)
Async XLA Ops:
  0.0 88.4 %copy-start = (bf16[4,128,2048]{2,1,0:T(8,128)(2,1)S(1)}, bf16[4,128,2048]{2,1,0:T(8,128)(2,1)}, u32[]{:S(2)}) copy-start(bf16[4,128,2048]{2,1,0:T(8,128)(2,1)} %param.18) | copy-start | bytes 6291460
  0.0 47.7 %copy-start.4 = (s32[64]{0:T(128)S(1)}, s32[64]{0:T(128)}, u32[]{:S(2)}) copy-start(s32[64]{0:T(128)} %param.19) | copy-start | bytes 772
  0.0 50.4 %copy-start.1 = (bf16[4,2048]{1,0:T(4,128)(2,1)S(1)}, bf16[4,2048]{1,0:T(4,128)(2,1)}, u32[]{:S(2)}) copy-start(bf16[4,2048]{1,0:T(4,128)(2,1)} %param.15) | copy-start | bytes 49156
  0.0 70.1 %copy-start.2 = (bf16[4,2048]{1,0:T(4,128)(2,1)S(1)}, bf16[4,2048]{1,0:T(4,128)(2,1)}, u32[]{:S(2)}) copy-start(bf16[4,2048]{1,0:T(4,128)(2,1)} %param.16) | copy-start | bytes 49156
  25.2 64.3 %copy-start.5 = (s32[64,6]{0,1:T(8,128)S(1)}, s32[64,6]{0,1:T(8,128)}, u32[]{:S(2)}) copy-start(s32[64,6]{0,1:T(8,128)} %param.20) | copy-start | bytes 4612
  25.2 64.5 %copy-start.3 = (f32[2048]{0:T(1024)S(1)}, f32[2048]{0:T(1024)}, u32[]{:S(2)}) copy-start(f32[2048]{0:T(1024)} %param.22) | copy-start | bytes 24580
  104.6 11.9 %copy-start.6 = (f32[64,6]{0,1:T(8,128)S(1)}, f32[64,6]{0,1:T(8,128)}, u32[]{:S(2)}) copy-start(f32[64,6]{0,1:T(8,128)} %param.21) | copy-start | bytes 4612
  112.9 13.5 %all-to-all-start.1 = ((f32[16,2,2048]{2,1,0:T(2,128)}), f32[16,2,2048]{2,1,0:T(2,128)S(1)}, u32[]{:S(2)}, u32[]{:S(2)}) async-start(f32[16,2,2048]{2,1,0:T(2,128)} %copy.27), calls=%async_computation.1 | async-start | bytes 524288 | tf_op jit(solution)/shard_map/all_to_all | solution.py:106
where the time goes:
time: 128 us; the launch traced here: 127 us
  blocking collectives  90.9 us (71%)
  matrix products  16.8 us (13%)
  waiting for transfers between devices  9.8 us (8%)
  local copies, waits for them, and re-layouts  5.58 us (4%)
  starting transfers between devices  3.53 us (3%)
    all_gather x1, blocking collectives, body(): lax.all_gather(queries, ('expert', 'beam'), axis=0, tiled=True)  24.2 us
    all_gather x1, blocking collectives, body(): lax.all_gather(new_values, ('expert', 'beam'), axis=0, tiled=True)  19.4 us
    all_gather x1, blocking collectives, body(): lax.all_gather(new_keys, ('expert', 'beam'), axis=0, tiled=True)  18.4 us
    all_gather x1, blocking collectives, body(): lax.all_gather(resid, ('expert', 'beam'), axis=0, tiled=True)  18.2 us
    all_to_all x1, blocking collectives, body(): lax.all_to_all(outgoing, 'expert', split_axis=0, concat_axis=0, tiled=True)  10.7 us
    all_to_all x1, waiting for transfers between devices, body(): lax.all_to_all(summed, 'expert', split_axis=0, concat_axis=0, tiled=True)  9.8 us
    reshape x1, local copies, waits for them, and re-layouts, attend(): key_heads = key_cache.reshape(slots, positions, head_count, head_size)  3.97 us
    dot_general x1, matrix products, expert_rows_out(): return jnp.dot(inner, w_down[0], preferred_element_type=jnp.float32)  3.72 us
  transfers between devices with their start and end apart: 1, of which 1 were waited for; matrix products, arithmetic and copies ran while one was open for 0% of the time, Pallas kernels for 0%

commit v1 on v0

v1 whole, which is shorter than its diff:
```python
import functools
import math

import jax
import jax.numpy as jnp
from jax import lax
from jax.experimental import pallas as pl
from jax.experimental.pallas import tpu as pltpu
from jax.sharding import PartitionSpec as P

HEAD_DIM = 128
LANES = 128
PIECES = 4
F32 = jnp.float32
BF16 = jnp.bfloat16


def flip(index, bit):
    return index + bit * (1 - 2 * lax.rem(lax.div(index, bit), 2))


def layer_kernel(
    cfg,
    parent,
    route_ids,
    route_weights,
    gain,
    queries,
    new_keys,
    new_values,
    resid,
    key_cache,
    value_cache,
    w_gate,
    w_up,
    w_down,
    out,
    all_q,
    all_s,
    all_vr,
    own_key,
    keys,
    values,
    gate,
    up,
    down,
    mixed_ref,
    hidden_ref,
    spread,
    disp,
    arrived,
    tokens,
    gate_acc,
    up_acc,
    piece_ref,
    outgoing,
    returned,
    own_sem,
    key_sem,
    value_sem,
    weight_sem,
    send_sem,
    q_sem,
    s_sem,
    vr_sem,
    token_sem,
    back_sem,
):
    experts, beams, minor, capacity = cfg
    count = experts * beams
    major = count // minor
    rows, width = hidden_ref.shape
    heads = width // HEAD_DIM
    chosen = route_ids.shape[1]
    scale = 1.0 / math.sqrt(HEAD_DIM)
    me = lax.axis_index("expert") * beams + lax.axis_index("beam")
    high, low = lax.div(me, minor), lax.rem(me, minor)

    def place(index):
        return {"expert": lax.div(index, beams), "beam": lax.rem(index, beams)}

    def other(step):
        return lax.rem(me + step, count)

    own_copies = [
        pltpu.make_async_copy(queries, all_q.at[me], own_sem.at[0]),
        pltpu.make_async_copy(new_keys, own_key, own_sem.at[1]),
        pltpu.make_async_copy(new_values, all_vr.at[me, 0], own_sem.at[2]),
        pltpu.make_async_copy(resid, all_vr.at[me, 1], own_sem.at[3]),
    ]
    for copy in own_copies:
        copy.start()
    barrier = pltpu.get_barrier_semaphore()
    for step in range(1, count):
        pl.semaphore_signal(
            barrier,
            inc=1,
            device_id=place(other(step)),
            device_id_type=pl.DeviceIdType.MESH,
        )
    key_copies = []
    value_copies = []
    for slot in range(rows):
        key_copies.append(
            pltpu.make_async_copy(key_cache.at[slot], keys.at[slot], key_sem.at[slot])
        )
    for slot in range(rows):
        value_copies.append(
            pltpu.make_async_copy(value_cache.at[slot], values.at[slot], value_sem.at[slot])
        )
    for copy in key_copies + value_copies:
        copy.start()
    weight_waits = []
    for number, (source, target) in enumerate(((w_gate, gate), (w_up, up), (w_down, down))):
        depth = target.shape[0]
        part = depth // 4
        for chunk in range(4):
            span = pl.ds(chunk * part, part)
            pltpu.make_async_copy(
                source.at[0, span, :], target.at[span, :], weight_sem.at[number]
            ).start()
        weight_waits.append(pltpu.make_async_copy(target, target, weight_sem.at[number]))

    def push(buffer, block, target, send, receive):
        pltpu.make_async_remote_copy(
            src_ref=buffer.at[block],
            dst_ref=buffer.at[block],
            send_sem=send,
            recv_sem=receive.at[block],
            device_id=place(target),
            device_id_type=pl.DeviceIdType.MESH,
        ).start()

    def landed(buffer, block, receive):
        pltpu.make_async_copy(buffer.at[block], buffer.at[block], receive.at[block]).wait()

    bits = []
    bit = minor // 2
    while bit >= 1:
        bits.append(bit)
        bit //= 2


    def block_of(step, flips):
        lane = low
        for b in flips:
            lane = flip(lane, b)
        return lax.rem(high + step, major) * minor + lane

    def subsets(names):
        found = [()]
        for b in names:
            found = found + [f + (b,) for f in found]
        return found

    def push_own(buffer, send, receive):
        for step in range(1, major):
            push(buffer, me, block_of(step, ()), send, receive)
        for b in bits:
            push(buffer, me, flip(me, b), send, receive)

    def forward_line(buffer, send, receive):
        for step in range(1, major):
            block = block_of(step, ())
            landed(buffer, block, receive)
            for b in bits:
                push(buffer, block, flip(me, b), send, receive)

    def forward_level(buffer, level, send, receive):
        for flips in subsets(bits[:level]):
            for step in range(major):
                block = block_of(step, flips + (bits[level],))
                landed(buffer, block, receive)
                for b in bits[level + 1 :]:
                    push(buffer, block, flip(me, b), send, receive)

    first_slot = me * rows

    def find_child(beam, found):
        origin = parent[beam]
        return tuple(
            jnp.where(origin == first_slot + slot, beam, found[slot]) for slot in range(rows)
        )

    own_copies[0].wait()
    own_copies[1].wait()
    product = all_q[me].astype(F32) * own_key[...].astype(F32)
    lane = lax.broadcasted_iota(jnp.int32, (rows, LANES), 1)
    self_rows = jnp.zeros((rows, LANES), F32)
    for head in range(heads):
        total = jnp.sum(
            product[:, head * HEAD_DIM : (head + 1) * HEAD_DIM], axis=1, keepdims=True
        )
        self_rows = jnp.where(lane == head, total * scale, self_rows)
    all_s[me] = self_rows
    own_copies[2].wait()
    own_copies[3].wait()

    pl.semaphore_wait(barrier, count - 1)
    push_own(all_q, send_sem.at[0], q_sem)
    push_own(all_s, send_sem.at[1], s_sem)
    push_own(all_vr, send_sem.at[2], vr_sem)
    child = lax.fori_loop(
        0, parent.shape[0], find_child, tuple(jnp.int32(0) for _ in range(rows))
    )

    places = experts * capacity

    def slot_tables(shape, dimension):
        numbers = lax.broadcasted_iota(jnp.int32, shape, dimension)
        expert_of, rank_of = lax.div(numbers, capacity), lax.rem(numbers, capacity)
        ranks = jnp.zeros(shape, jnp.int32)
        placed, weights = [], []
        for slot in range(rows):
            named = jnp.zeros(shape, jnp.int32)
            weight = jnp.zeros(shape, F32)
            for pick in range(chosen):
                hit = expert_of == route_ids[first_slot + slot, pick]
                named = jnp.where(hit, 1, named)
                weight = weight + jnp.where(hit, route_weights[first_slot + slot, pick], 0.0)
            mine = (named == 1) & (ranks == rank_of)
            placed.append(jnp.where(mine, 1.0, 0.0))
            weights.append(jnp.where(mine, weight, 0.0))
            ranks = ranks + named
        return placed, weights

    placed, _ = slot_tables((places, 1), 0)
    lanes_of_places = -(-places // LANES) * LANES
    _, lane_weights = slot_tables((1, lanes_of_places), 1)
    row_number = lax.broadcasted_iota(jnp.int32, (rows, lanes_of_places), 0)
    combine = jnp.zeros((rows, lanes_of_places), F32)
    for slot in range(rows):
        combine = jnp.where(row_number == slot, lane_weights[slot], combine)

    forward_line(all_q, send_sem.at[0], q_sem)
    forward_line(all_s, send_sem.at[1], s_sem)
    levels = len(bits)
    for level in range(levels):
        forward_level(all_q, level, send_sem.at[0], q_sem)
        forward_level(all_s, level, send_sem.at[1], s_sem)
        if level == 0:
            forward_line(all_vr, send_sem.at[2], vr_sem)

    head_mask = lax.broadcasted_iota(jnp.int32, (heads, width), 0) == lax.div(
        lax.broadcasted_iota(jnp.int32, (heads, width), 1), HEAD_DIM
    )
    self_mask = lax.broadcasted_iota(jnp.int32, (heads, LANES), 0) == lax.broadcasted_iota(
        jnp.int32, (heads, LANES), 1
    )

    def pick(block, row):
        block = block.astype(F32)
        chosen_row = lax.broadcasted_iota(jnp.int32, block.shape, 0) == row
        return jnp.sum(jnp.where(chosen_row, block, 0.0), axis=0, keepdims=True)

    probs, selfs, denominators = [], [], []
    for slot in range(rows):
        device, row = lax.div(child[slot], rows), lax.rem(child[slot], rows)
        query = pick(all_q[device], row)
        spread_query = jnp.where(head_mask, query, 0.0).astype(BF16)
        key_copies[slot].wait()
        scores = (
            lax.dot_general(
                spread_query,
                keys[slot],
                (((1,), (1,)), ((), ())),
                preferred_element_type=F32,
            )
            * scale
        )
        self_score = jnp.sum(
            jnp.where(self_mask, pick(all_s[device], row), 0.0), axis=1, keepdims=True
        )
        peak = jnp.maximum(jnp.max(scores, axis=1, keepdims=True), self_score)
        expo = jnp.exp(scores - peak)
        self_expo = jnp.exp(self_score - peak)
        denominators.append(jnp.sum(expo, axis=1, keepdims=True) + self_expo)
        probs.append(expo.astype(BF16))
        selfs.append(self_expo.astype(BF16).astype(F32))
    for slot in range(rows):
        value_copies[slot].wait()
        mixed_ref[slot] = jnp.dot(probs[slot], values[slot], preferred_element_type=F32)
    for level in range(levels):
        forward_level(all_vr, level, send_sem.at[2], vr_sem)

    gains = gain[...]
    normed = []
    for slot in range(rows):
        device, row = lax.div(child[slot], rows), lax.rem(child[slot], rows)
        new_value = pick(all_vr[device, 0], row)
        residual = pick(all_vr[device, 1], row)
        mixed = (mixed_ref[slot] + selfs[slot] * new_value) / denominators[slot]
        attended = jnp.sum(jnp.where(head_mask, mixed, 0.0), axis=0, keepdims=True)
        hidden = residual + attended.astype(BF16).astype(F32)
        hidden_ref[pl.ds(slot, 1), :] = hidden
        mean = jnp.mean(hidden * hidden, axis=1, keepdims=True)
        row_normed = (hidden * lax.rsqrt(mean + 1e-06) * gains).astype(BF16)
        normed.append(row_normed.astype(F32))
    total = placed[0] * normed[0]
    for slot in range(1, rows):
        total = total + placed[slot] * normed[slot]
    spread[...] = total
    for expert in range(experts):
        disp[expert] = spread[pl.ds(expert * capacity, capacity), :].astype(BF16)
    for step in range(1, count):
        target = other(step)
        pltpu.make_async_remote_copy(
            src_ref=disp.at[lax.div(target, beams)],
            dst_ref=arrived.at[me],
            send_sem=send_sem.at[3],
            recv_sem=token_sem.at[me],
            device_id=place(target),
            device_id_type=pl.DeviceIdType.MESH,
        ).start()
    arrived[me] = disp[lax.div(me, beams)]
    for source in range(count):

        @pl.when(me != source)
        def _():
            landed(arrived, source, token_sem)

        tokens[pl.ds(source * capacity, capacity), :] = arrived[source].astype(F32)

    weight_waits[0].wait()
    weight_waits[1].wait()
    chunk = 256 if width % 256 == 0 else LANES
    gate_acc[...] = jnp.zeros_like(gate_acc)
    up_acc[...] = jnp.zeros_like(up_acc)

    def gate_up(step, carry):
        span = pl.ds(pl.multiple_of(step * chunk, chunk), chunk)
        left = tokens[:, span].astype(BF16)
        gate_acc[...] += jnp.dot(left, gate[span, :], preferred_element_type=F32)
        up_acc[...] += jnp.dot(left, up[span, :], preferred_element_type=F32)
        return carry

    lax.fori_loop(0, width // chunk, gate_up, 0)
    activation = gate_acc[...]
    inner = (activation / (1.0 + jnp.exp(-activation)) * up_acc[...]).astype(BF16)
    weight_waits[2].wait()
    part = width // PIECES
    for piece in range(PIECES):
        piece_ref[...] = jnp.dot(
            inner, down[:, piece * part : (piece + 1) * part], preferred_element_type=F32
        )
        for source in range(count):
            outgoing[piece, source] = piece_ref[pl.ds(source * capacity, capacity), :].astype(BF16)
        for step in range(1, count):
            target = other(step)
            pltpu.make_async_remote_copy(
                src_ref=outgoing.at[piece, target],
                dst_ref=returned.at[piece, me],
                send_sem=send_sem.at[4 + piece],
                recv_sem=back_sem.at[piece],
                device_id=place(target),
                device_id_type=pl.DeviceIdType.MESH,
            ).start()
        returned[piece, me] = outgoing[piece, me]

    for piece in range(PIECES):
        rest = returned.at[piece, pl.ds(0, count - 1)]
        pltpu.make_async_copy(rest, rest, back_sem.at[piece]).wait()
        columns = pl.ds(piece * part, part)
        sums = hidden_ref[:, columns]
        for source in range(count):
            block = returned[piece, source].astype(F32)
            for rank in range(capacity):
                at = (source // beams) * capacity + rank
                sums = sums + combine[:, at : at + 1] * block[rank : rank + 1, :]
        out[:, columns] = sums.astype(out.dtype)

    for number, buffer in enumerate((all_q, all_s, all_vr, arrived)):
        sent = buffer.at[pl.ds(0, count - 1)]
        pltpu.make_async_copy(sent, sent, send_sem.at[number]).wait()
    for piece in range(PIECES):
        sent = outgoing.at[piece, pl.ds(0, count - 1)]
        pltpu.make_async_copy(sent, sent, send_sem.at[4 + piece]).wait()


def body(
    queries,
    new_keys,
    new_values,
    resid,
    key_cache,
    value_cache,
    parent,
    route_ids,
    route_weights,
    norm_gain,
    w_gate,
    w_up,
    w_down,
):
    rows, width = queries.shape
    positions = key_cache.shape[1]
    hidden_units = w_gate.shape[2]
    experts, beams = lax.axis_size("expert"), lax.axis_size("beam")
    count = experts * beams
    minor = beams
    while minor < 4 and beams == 1 and experts % (2 * minor) == 0:
        minor *= 2
    capacity = max(2, -(-rows * route_ids.shape[1] // experts))
    heads = width // HEAD_DIM
    part = width // PIECES
    vmem = pltpu.VMEM
    smem_spec = pl.BlockSpec(memory_space=pltpu.SMEM)
    any_spec = pl.BlockSpec(memory_space=pl.ANY)
    vmem_spec = pl.BlockSpec(memory_space=pltpu.VMEM)
    dma = pltpu.SemaphoreType.DMA
    return pl.pallas_call(
        functools.partial(layer_kernel, (experts, beams, minor, capacity)),
        out_shape=jax.ShapeDtypeStruct((rows, width), BF16),
        in_specs=[smem_spec] * 3 + [vmem_spec] + [any_spec] * 9,
        out_specs=vmem_spec,
        scratch_shapes=[
            vmem((count, rows, width), BF16),
            vmem((count, rows, LANES), F32),
            vmem((count, 2, rows, width), BF16),
            vmem((rows, width), BF16),
            vmem((rows, positions, width), BF16),
            vmem((rows, positions, width), BF16),
            vmem((width, hidden_units), BF16),
            vmem((width, hidden_units), BF16),
            vmem((hidden_units, width), BF16),
            vmem((rows, heads, width), F32),
            vmem((rows, width), F32),
            vmem((experts * capacity, width), F32),
            vmem((experts, capacity, width), BF16),
            vmem((count, capacity, width), BF16),
            vmem((count * capacity, width), F32),
            vmem((count * capacity, hidden_units), F32),
            vmem((count * capacity, hidden_units), F32),
            vmem((count * capacity, part), F32),
            vmem((PIECES, count, capacity, part), BF16),
            vmem((PIECES, count, capacity, part), BF16),
            dma((4,)),
            dma((rows,)),
            dma((rows,)),
            dma((3,)),
            dma((4 + PIECES,)),
            dma((count,)),
            dma((count,)),
            dma((count,)),
            dma((count,)),
            dma((PIECES,)),
        ],
        compiler_params=pltpu.CompilerParams(collective_id=0, has_side_effects=True),
    )(
        parent,
        route_ids,
        route_weights,
        norm_gain[None, :],
        queries,
        new_keys,
        new_values,
        resid,
        key_cache,
        value_cache,
        w_gate,
        w_up,
        w_down,
    )


def solution(mesh):
    return jax.shard_map(
        body,
        mesh=mesh,
        in_specs=(
            P(("groups", "expert", "beam"), None),
            P(("groups", "expert", "beam"), None),
            P(("groups", "expert", "beam"), None),
            P(("groups", "expert", "beam"), None),
            P(("groups", "expert", "beam"), None, None),
            P(("groups", "expert", "beam"), None, None),
            P("groups"),
            P("groups", None),
            P("groups", None),
            P(),
            P("expert", None, "beam"),
            P("expert", None, "beam"),
            P("expert", "beam", None),
        ),
        out_specs=P(("groups", "expert", "beam"), None),
        check_vma=False,
    )
```

time: 128 us -> 40.7 us (0.32)
  blocking collectives: 90.9 us -> 0 us
  Pallas kernels: 0 us -> 36.2 us
  matrix products: 16.8 us -> 0 us
  waiting for transfers between devices: 9.8 us -> 0 us
  starting transfers between devices: 3.53 us -> 0 us
  local copies, waits for them, and re-layouts: 5.58 us -> 4.08 us
    all_gather x4 -> x0, blocking collectives: 80.2 us -> none  [the longest x1 24.2 us: body(): lax.all_gather(queries, ('expert', 'beam'), axis=0, tiled=True)]
    pallas_call x0 -> x1, Pallas kernels: none -> 36.2 us  [body(): pl.pallas_call(functools.partial(layer_kernel, (experts, beams, minor, ca...]
    dot_general x11 -> x0, matrix products: 16.8 us -> none  [the longest x1 3.72 us: expert_rows_out(): return jnp.dot(inner, w_down[0], preferred_element_type=jnp.float32)]
    all_to_all x1 -> x0, blocking collectives: 10.7 us -> none  [body(): lax.all_to_all(outgoing, 'expert', split_axis=0, concat_axis=0, tiled=True)]
    all_to_all x1 -> x0, waiting for transfers between devices: 9.8 us -> none  [body(): lax.all_to_all(summed, 'expert', split_axis=0, concat_axis=0, tiled=True)]
    reshape x3 -> x0, local copies, waits for them, and re-layouts: 4.05 us -> none  [the longest x1 3.97 us: attend(): key_heads = key_cache.reshape(slots, positions, head_count, head_size)]
    unnamed x18 -> x3, local copies, waits for them, and re-layouts: 0.29 us -> 4.08 us
    all_to_all x1 -> x0, starting transfers between devices: 3.53 us -> none  [body(): lax.all_to_all(summed, 'expert', split_axis=0, concat_axis=0, tiled=True)]
  transfers between devices with their start and end apart: 1 -> 0, of which waited for: 1 -> 0; matrix products, arithmetic and copies ran while one was open for 0% -> 0% of each run, Pallas kernels for 0% -> 0%
where the time goes in v1:
time: 40.7 us; the launch traced here: 40.3 us
  Pallas kernels  36.2 us (89%)
  local copies, waits for them, and re-layouts  4.08 us (10%)
    pallas_call x1, Pallas kernels, body(): pl.pallas_call(functools.partial(layer_kernel, (experts, beams, minor, ca...  36.2 us
    unnamed x3, local copies, waits for them, and re-layouts  4.08 us

profile of v1, /device:TPU:0, one launch (start us, length us, event | category | flops | bytes accessed | tf_op | source)
XLA Modules:
  0.0 40.3 jit_solution(12099292707335141284)
XLA Ops:
  0.0 1.4 %copy.14.route_ids = s32[64,6]{1,0:T(8,128)} copy(s32[64,6]{0,1:T(8,128)} %param.20) | data formatting | bytes 3072 | tf_op args[7]
  1.4 1.4 %copy.15.route_weights = f32[64,6]{1,0:T(8,128)} copy(f32[64,6]{0,1:T(8,128)} %param.21) | data formatting | bytes 3072 | tf_op args[8]
  2.8 36.2 %shard_map.127 = bf16[4,2048]{1,0:T(4,128)(2,1)} custom-call(s32[64]{0:T(128)} %parent.1, s32[64,6]{1,0:T(8,128)} %copy.14.route_ids, f32[64,6]{1,0:T(8,128)} %copy.15.route_weights, f32[1,2048]{1,0:T(1,128)} %bitcast.1, bf16[4,2048]{1,0:T(4,128)(2,1)} %queries.1, bf16[4,2048]{1,0:T(4,128)(2,1)} %new_keys.1, bf16[4,2048]{1,0:T(4,128)(2,1)} %new_values.1, ...), custom_call_target="tpu_custom_call" | custom-call | tf_op jit(solution)/shard_map/pallas_call | solution.py:411
  39.0 1.3 %copy.17 = bf16[4,2048]{1,0:T(4,128)(2,1)} copy(bf16[4,2048]{1,0:T(4,128)(2,1)} %shard_map.127) | data formatting | bytes 32768

commit v2 on v1

--- a/solution.py
+++ b/solution.py
@@ -21,10 +21,10 @@
 
 def layer_kernel(
     cfg,
-    parent,
-    route_ids,
-    route_weights,
-    gain,
+    parent_in,
+    route_ids_in,
+    route_weights_in,
+    gain_in,
     queries,
     new_keys,
     new_values,
@@ -35,6 +35,10 @@
     w_up,
     w_down,
     out,
+    parent,
+    route_ids,
+    route_weights,
+    gain,
     all_q,
     all_s,
     all_vr,
@@ -71,7 +75,7 @@
     major = count // minor
     rows, width = hidden_ref.shape
     heads = width // HEAD_DIM
-    chosen = route_ids.shape[1]
+    chosen = route_ids.shape[0]
     scale = 1.0 / math.sqrt(HEAD_DIM)
     me = lax.axis_index("expert") * beams + lax.axis_index("beam")
     high, low = lax.div(me, minor), lax.rem(me, minor)
@@ -88,16 +92,35 @@
         pltpu.make_async_copy(new_values, all_vr.at[me, 0], own_sem.at[2]),
         pltpu.make_async_copy(resid, all_vr.at[me, 1], own_sem.at[3]),
     ]
-    for copy in own_copies:
-        copy.start()
+    small_copies = [
+        pltpu.make_async_copy(parent_in, parent, own_sem.at[4]),
+        pltpu.make_async_copy(route_ids_in, route_ids, own_sem.at[5]),
+        pltpu.make_async_copy(route_weights_in, route_weights, own_sem.at[6]),
+        pltpu.make_async_copy(gain_in, gain, own_sem.at[7]),
+    ]
+    bits = []
+    bit = minor // 2
+    while bit >= 1:
+        bits.append(bit)
+        bit //= 2
+
+    def block_of(step, flips):
+        lane = low
+        for b in flips:
+            lane = flip(lane, b)
+        return lax.rem(high + step, major) * minor + lane
+
     barrier = pltpu.get_barrier_semaphore()
-    for step in range(1, count):
+    greeted = [block_of(step, ()) for step in range(1, major)] + [flip(me, b) for b in bits]
+    for target in greeted:
         pl.semaphore_signal(
             barrier,
             inc=1,
-            device_id=place(other(step)),
+            device_id=place(target),
             device_id_type=pl.DeviceIdType.MESH,
         )
+    for copy in own_copies + small_copies:
+        copy.start()
     key_copies = []
     value_copies = []
     for slot in range(rows):
@@ -134,19 +157,6 @@
     def landed(buffer, block, receive):
         pltpu.make_async_copy(buffer.at[block], buffer.at[block], receive.at[block]).wait()
 
-    bits = []
-    bit = minor // 2
-    while bit >= 1:
-        bits.append(bit)
-        bit //= 2
-
-
-    def block_of(step, flips):
-        lane = low
-        for b in flips:
-            lane = flip(lane, b)
-        return lax.rem(high + step, major) * minor + lane
-
     def subsets(names):
         found = [()]
         for b in names:
@@ -159,16 +169,16 @@
         for b in bits:
             push(buffer, me, flip(me, b), send, receive)
 
-    def forward_line(buffer, send, receive):
-        for step in range(1, major):
+    def forward_line(buffer, send, receive, steps=None):
+        for step in range(1, major) if steps is None else steps:
             block = block_of(step, ())
             landed(buffer, block, receive)
             for b in bits:
                 push(buffer, block, flip(me, b), send, receive)
 
-    def forward_level(buffer, level, send, receive):
+    def forward_level(buffer, level, send, receive, steps=None):
         for flips in subsets(bits[:level]):
-            for step in range(major):
+            for step in range(major) if steps is None else steps:
                 block = block_of(step, flips + (bits[level],))
                 landed(buffer, block, receive)
                 for b in bits[level + 1 :]:
@@ -183,6 +193,8 @@
         )
 
     own_copies[0].wait()
+    pl.semaphore_wait(barrier, len(greeted))
+    push_own(all_q, send_sem.at[0], q_sem)
     own_copies[1].wait()
     product = all_q[me].astype(F32) * own_key[...].astype(F32)
     lane = lax.broadcasted_iota(jnp.int32, (rows, LANES), 1)
@@ -195,11 +207,10 @@
     all_s[me] = self_rows
     own_copies[2].wait()
     own_copies[3].wait()
-
-    pl.semaphore_wait(barrier, count - 1)
-    push_own(all_q, send_sem.at[0], q_sem)
     push_own(all_s, send_sem.at[1], s_sem)
     push_own(all_vr, send_sem.at[2], vr_sem)
+    for copy in small_copies:
+        copy.wait()
     child = lax.fori_loop(
         0, parent.shape[0], find_child, tuple(jnp.int32(0) for _ in range(rows))
     )
@@ -215,9 +226,9 @@
             named = jnp.zeros(shape, jnp.int32)
             weight = jnp.zeros(shape, F32)
             for pick in range(chosen):
-                hit = expert_of == route_ids[first_slot + slot, pick]
+                hit = expert_of == route_ids[pick, first_slot + slot]
                 named = jnp.where(hit, 1, named)
-                weight = weight + jnp.where(hit, route_weights[first_slot + slot, pick], 0.0)
+                weight = weight + jnp.where(hit, route_weights[pick, first_slot + slot], 0.0)
             mine = (named == 1) & (ranks == rank_of)
             placed.append(jnp.where(mine, 1.0, 0.0))
             weights.append(jnp.where(mine, weight, 0.0))
@@ -236,10 +247,14 @@
     forward_line(all_s, send_sem.at[1], s_sem)
     levels = len(bits)
     for level in range(levels):
-        forward_level(all_q, level, send_sem.at[0], q_sem)
+        if level == 0:
+            for step in range(major):
+                forward_level(all_q, level, send_sem.at[0], q_sem, (step,))
+                if step > 0:
+                    forward_line(all_vr, send_sem.at[2], vr_sem, (step,))
+        else:
+            forward_level(all_q, level, send_sem.at[0], q_sem)
         forward_level(all_s, level, send_sem.at[1], s_sem)
-        if level == 0:
-            forward_line(all_vr, send_sem.at[2], vr_sem)
 
     head_mask = lax.broadcasted_iota(jnp.int32, (heads, width), 0) == lax.div(
         lax.broadcasted_iota(jnp.int32, (heads, width), 1), HEAD_DIM
@@ -300,45 +315,47 @@
     for slot in range(1, rows):
         total = total + placed[slot] * normed[slot]
     spread[...] = total
-    for expert in range(experts):
-        disp[expert] = spread[pl.ds(expert * capacity, capacity), :].astype(BF16)
-    for step in range(1, count):
-        target = other(step)
-        pltpu.make_async_remote_copy(
-            src_ref=disp.at[lax.div(target, beams)],
-            dst_ref=arrived.at[me],
-            send_sem=send_sem.at[3],
-            recv_sem=token_sem.at[me],
-            device_id=place(target),
-            device_id_type=pl.DeviceIdType.MESH,
-        ).start()
-    arrived[me] = disp[lax.div(me, beams)]
-    for source in range(count):
-
-        @pl.when(me != source)
-        def _():
-            landed(arrived, source, token_sem)
-
-        tokens[pl.ds(source * capacity, capacity), :] = arrived[source].astype(F32)
-
-    weight_waits[0].wait()
-    weight_waits[1].wait()
-    chunk = 256 if width % 256 == 0 else LANES
-    gate_acc[...] = jnp.zeros_like(gate_acc)
-    up_acc[...] = jnp.zeros_like(up_acc)
-
-    def gate_up(step, carry):
-        span = pl.ds(pl.multiple_of(step * chunk, chunk), chunk)
-        left = tokens[:, span].astype(BF16)
-        gate_acc[...] += jnp.dot(left, gate[span, :], preferred_element_type=F32)
-        up_acc[...] += jnp.dot(left, up[span, :], preferred_element_type=F32)
-        return carry
-
-    lax.fori_loop(0, width // chunk, gate_up, 0)
+    part = width // PIECES
+    for piece in range(PIECES):
+        columns = pl.ds(piece * part, part)
+        for expert in range(experts):
+            disp[piece, expert] = spread[pl.ds(expert * capacity, capacity), columns].astype(BF16)
+        for step in range(1, count):
+            target = other(step)
+            pltpu.make_async_remote_copy(
+                src_ref=disp.at[piece, lax.div(target, beams)],
+                dst_ref=arrived.at[piece, me],
+                send_sem=send_sem.at[3 + piece],
+                recv_sem=token_sem.at[piece],
+                device_id=place(target),
+                device_id_type=pl.DeviceIdType.MESH,
+            ).start()
+        arrived[piece, me] = disp[piece, lax.div(me, beams)]
+
+    def rest_of(buffer, piece):
+        return buffer.at[piece, pl.ds(0, count - 1)]
+
+    for piece in range(PIECES):
+        rest = rest_of(arrived, piece)
+        pltpu.make_async_copy(rest, rest, token_sem.at[piece]).wait()
+        for source in range(count):
+            tokens[pl.ds(source * capacity, capacity), :] = arrived[piece, source].astype(F32)
+        if piece == 0:
+            weight_waits[0].wait()
+            weight_waits[1].wait()
+        span = pl.ds(piece * part, part)
+        left = tokens[...].astype(BF16)
+        gate_part = jnp.dot(left, gate[span, :], preferred_element_type=F32)
+        up_part = jnp.dot(left, up[span, :], preferred_element_type=F32)
+        if piece == 0:
+            gate_acc[...] = gate_part
+            up_acc[...] = up_part
+        else:
+            gate_acc[...] += gate_part
+            up_acc[...] += up_part
     activation = gate_acc[...]
     inner = (activation / (1.0 + jnp.exp(-activation)) * up_acc[...]).astype(BF16)
     weight_waits[2].wait()
-    part = width // PIECES
     for piece in range(PIECES):
         piece_ref[...] = jnp.dot(
             inner, down[:, piece * part : (piece + 1) * part], preferred_element_type=F32
@@ -350,7 +367,7 @@
             pltpu.make_async_remote_copy(
                 src_ref=outgoing.at[piece, target],
                 dst_ref=returned.at[piece, me],
-                send_sem=send_sem.at[4 + piece],
+                send_sem=send_sem.at[3 + PIECES + piece],
                 recv_sem=back_sem.at[piece],
                 device_id=place(target),
                 device_id_type=pl.DeviceIdType.MESH,
@@ -358,7 +375,7 @@
         returned[piece, me] = outgoing[piece, me]
 
     for piece in range(PIECES):
-        rest = returned.at[piece, pl.ds(0, count - 1)]
+        rest = rest_of(returned, piece)
         pltpu.make_async_copy(rest, rest, back_sem.at[piece]).wait()
         columns = pl.ds(piece * part, part)
         sums = hidden_ref[:, columns]
@@ -369,12 +386,13 @@
                 sums = sums + combine[:, at : at + 1] * block[rank : rank + 1, :]
         out[:, columns] = sums.astype(out.dtype)
 
-    for number, buffer in enumerate((all_q, all_s, all_vr, arrived)):
+    for number, buffer in enumerate((all_q, all_s, all_vr)):
         sent = buffer.at[pl.ds(0, count - 1)]
         pltpu.make_async_copy(sent, sent, send_sem.at[number]).wait()
     for piece in range(PIECES):
-        sent = outgoing.at[piece, pl.ds(0, count - 1)]
-        pltpu.make_async_copy(sent, sent, send_sem.at[4 + piece]).wait()
+        for number, buffer in ((3, arrived), (3 + PIECES, outgoing)):
+            sent = rest_of(buffer, piece)
+            pltpu.make_async_copy(sent, sent, send_sem.at[number + piece]).wait()
 
 
 def body(
@@ -404,16 +422,20 @@
     heads = width // HEAD_DIM
     part = width // PIECES
     vmem = pltpu.VMEM
-    smem_spec = pl.BlockSpec(memory_space=pltpu.SMEM)
+    smem = pltpu.SMEM
     any_spec = pl.BlockSpec(memory_space=pl.ANY)
     vmem_spec = pl.BlockSpec(memory_space=pltpu.VMEM)
     dma = pltpu.SemaphoreType.DMA
     return pl.pallas_call(
         functools.partial(layer_kernel, (experts, beams, minor, capacity)),
         out_shape=jax.ShapeDtypeStruct((rows, width), BF16),
-        in_specs=[smem_spec] * 3 + [vmem_spec] + [any_spec] * 9,
+        in_specs=[any_spec] * 13,
         out_specs=vmem_spec,
         scratch_shapes=[
+            smem(parent.shape, jnp.int32),
+            smem(route_ids.shape[::-1], jnp.int32),
+            smem(route_weights.shape[::-1], F32),
+            vmem((1, width), F32),
             vmem((count, rows, width), BF16),
             vmem((count, rows, LANES), F32),
             vmem((count, 2, rows, width), BF16),
@@ -426,30 +448,30 @@
             vmem((rows, heads, width), F32),
             vmem((rows, width), F32),
             vmem((experts * capacity, width), F32),
-            vmem((experts, capacity, width), BF16),
-            vmem((count, capacity, width), BF16),
-            vmem((count * capacity, width), F32),
+            vmem((PIECES, experts, capacity, part), BF16),
+            vmem((PIECES, count, capacity, part), BF16),
+            vmem((count * capacity, part), F32),
             vmem((count * capacity, hidden_units), F32),
             vmem((count * capacity, hidden_units), F32),
             vmem((count * capacity, part), F32),
             vmem((PIECES, count, capacity, part), BF16),
             vmem((PIECES, count, capacity, part), BF16),
-            dma((4,)),
+            dma((8,)),
             dma((rows,)),
             dma((rows,)),
             dma((3,)),
-            dma((4 + PIECES,)),
+            dma((3 + 2 * PIECES,)),
             dma((count,)),
             dma((count,)),
             dma((count,)),
-            dma((count,)),
+            dma((PIECES,)),
             dma((PIECES,)),
         ],
         compiler_params=pltpu.CompilerParams(collective_id=0, has_side_effects=True),
     )(
         parent,
-        route_ids,
-        route_weights,
+        route_ids.T,
+        route_weights.T,
         norm_gain[None, :],
         queries,
         new_keys,

time: 40.7 us -> 34.2 us (0.84)
  Pallas kernels: 36.2 us -> 32.6 us
  local copies, waits for them, and re-layouts: 4.08 us -> 1.33 us
    pallas_call x1, Pallas kernels: 36.2 us -> 32.6 us  [body(): pl.pallas_call(functools.partial(layer_kernel, (experts, beams, minor, ca...]
    unnamed x3 -> x1, local copies, waits for them, and re-layouts: 4.08 us -> 1.33 us
where the time goes in v2:
time: 34.2 us; the launch traced here: 34 us
  Pallas kernels  32.6 us (95%)
  local copies, waits for them, and re-layouts  1.33 us (4%)
    pallas_call x1, Pallas kernels, body(): pl.pallas_call(functools.partial(layer_kernel, (experts, beams, minor, ca...  32.6 us
    unnamed x1, local copies, waits for them, and re-layouts  1.33 us

profile of v2, /device:TPU:0, one launch (start us, length us, event | category | flops | bytes accessed | tf_op | source)
XLA Modules:
  0.0 34.0 jit_solution(16672801754092833123)
XLA Ops:
  0.0 32.6 %shard_map.127 = bf16[4,2048]{1,0:T(4,128)(2,1)} custom-call(s32[64]{0:T(128)} %parent_in.1, s32[6,64]{1,0:T(8,128)} %bitcast.4, f32[6,64]{1,0:T(8,128)} %bitcast.5, f32[1,2048]{1,0:T(1,128)} %bitcast.3, bf16[4,2048]{1,0:T(4,128)(2,1)} %queries.1, bf16[4,2048]{1,0:T(4,128)(2,1)} %new_keys.1, bf16[4,2048]{1,0:T(4,128)(2,1)} %new_values.1, ...), custom_call_target="tpu_custom_call" | custom-call | tf_op jit(solution)/shard_map/pallas_call | solution.py:429
  32.6 1.3 %copy.15 = bf16[4,2048]{1,0:T(4,128)(2,1)} copy(bf16[4,2048]{1,0:T(4,128)(2,1)} %shard_map.127) | data formatting | bytes 32768

commit v3 on v2

--- a/solution.py
+++ b/solution.py
@@ -133,6 +133,71 @@
         )
     for copy in key_copies + value_copies:
         copy.start()
+    def push(buffer, block, target, send, receive):
+        pltpu.make_async_remote_copy(
+            src_ref=buffer.at[block],
+            dst_ref=buffer.at[block],
+            send_sem=send,
+            recv_sem=receive.at[block],
+            device_id=place(target),
+            device_id_type=pl.DeviceIdType.MESH,
+        ).start()
+
+    def landed(buffer, block, receive):
+        pltpu.make_async_copy(buffer.at[block], buffer.at[block], receive.at[block]).wait()
+
+    def subsets(names):
+        found = [()]
+        for b in names:
+            found = found + [f + (b,) for f in found]
+        return found
+
+    def push_own(buffer, send, receive):
+        for step in range(1, major):
+            push(buffer, me, block_of(step, ()), send, receive)
+        for b in bits:
+            push(buffer, me, flip(me, b), send, receive)
+
+    def forward_line(buffer, send, receive, steps=None):
+        for step in range(1, major) if steps is None else steps:
+            block = block_of(step, ())
+            landed(buffer, block, receive)
+            for b in bits:
+                push(buffer, block, flip(me, b), send, receive)
+
+    def forward_level(buffer, level, send, receive, steps=None):
+        for flips in subsets(bits[:level]):
+            for step in range(major) if steps is None else steps:
+                block = block_of(step, flips + (bits[level],))
+                landed(buffer, block, receive)
+                for b in bits[level + 1 :]:
+                    push(buffer, block, flip(me, b), send, receive)
+
+    first_slot = me * rows
+
+    def find_child(beam, found):
+        origin = parent[beam]
+        return tuple(
+            jnp.where(origin == first_slot + slot, beam, found[slot]) for slot in range(rows)
+        )
+
+    own_copies[0].wait()
+    pl.semaphore_wait(barrier, len(greeted))
+    push_own(all_q, send_sem.at[0], q_sem)
+    own_copies[1].wait()
+    product = all_q[me].astype(F32) * own_key[...].astype(F32)
+    lane = lax.broadcasted_iota(jnp.int32, (rows, LANES), 1)
+    self_rows = jnp.zeros((rows, LANES), F32)
+    for head in range(heads):
+        total = jnp.sum(
+            product[:, head * HEAD_DIM : (head + 1) * HEAD_DIM], axis=1, keepdims=True
+        )
+        self_rows = jnp.where(lane == head, total * scale, self_rows)
+    all_s[me] = self_rows
+    own_copies[2].wait()
+    own_copies[3].wait()
+    push_own(all_s, send_sem.at[1], s_sem)
+    push_own(all_vr, send_sem.at[2], vr_sem)
     weight_waits = []
     for number, (source, target) in enumerate(((w_gate, gate), (w_up, up), (w_down, down))):
         depth = target.shape[0]
@@ -144,71 +209,6 @@
             ).start()
         weight_waits.append(pltpu.make_async_copy(target, target, weight_sem.at[number]))
 
-    def push(buffer, block, target, send, receive):
-        pltpu.make_async_remote_copy(
-            src_ref=buffer.at[block],
-            dst_ref=buffer.at[block],
-            send_sem=send,
-            recv_sem=receive.at[block],
-            device_id=place(target),
-            device_id_type=pl.DeviceIdType.MESH,
-        ).start()
-
-    def landed(buffer, block, receive):
-        pltpu.make_async_copy(buffer.at[block], buffer.at[block], receive.at[block]).wait()
-
-    def subsets(names):
-        found = [()]
-        for b in names:
-            found = found + [f + (b,) for f in found]
-        return found
-
-    def push_own(buffer, send, receive):
-        for step in range(1, major):
-            push(buffer, me, block_of(step, ()), send, receive)
-        for b in bits:
-            push(buffer, me, flip(me, b), send, receive)
-
-    def forward_line(buffer, send, receive, steps=None):
-        for step in range(1, major) if steps is None else steps:
-            block = block_of(step, ())
-            landed(buffer, block, receive)
-            for b in bits:
-                push(buffer, block, flip(me, b), send, receive)
-
-    def forward_level(buffer, level, send, receive, steps=None):
-        for flips in subsets(bits[:level]):
-            for step in range(major) if steps is None else steps:
-                block = block_of(step, flips + (bits[level],))
-                landed(buffer, block, receive)
-                for b in bits[level + 1 :]:
-                    push(buffer, block, flip(me, b), send, receive)
-
-    first_slot = me * rows
-
-    def find_child(beam, found):
-        origin = parent[beam]
-        return tuple(
-            jnp.where(origin == first_slot + slot, beam, found[slot]) for slot in range(rows)
-        )
-
-    own_copies[0].wait()
-    pl.semaphore_wait(barrier, len(greeted))
-    push_own(all_q, send_sem.at[0], q_sem)
-    own_copies[1].wait()
-    product = all_q[me].astype(F32) * own_key[...].astype(F32)
-    lane = lax.broadcasted_iota(jnp.int32, (rows, LANES), 1)
-    self_rows = jnp.zeros((rows, LANES), F32)
-    for head in range(heads):
-        total = jnp.sum(
-            product[:, head * HEAD_DIM : (head + 1) * HEAD_DIM], axis=1, keepdims=True
-        )
-        self_rows = jnp.where(lane == head, total * scale, self_rows)
-    all_s[me] = self_rows
-    own_copies[2].wait()
-    own_copies[3].wait()
-    push_own(all_s, send_sem.at[1], s_sem)
-    push_own(all_vr, send_sem.at[2], vr_sem)
     for copy in small_copies:
         copy.wait()
     child = lax.fori_loop(
@@ -248,10 +248,8 @@
     levels = len(bits)
     for level in range(levels):
         if level == 0:
-            for step in range(major):
-                forward_level(all_q, level, send_sem.at[0], q_sem, (step,))
-                if step > 0:
-                    forward_line(all_vr, send_sem.at[2], vr_sem, (step,))
+            forward_line(all_vr, send_sem.at[2], vr_sem)
+            forward_level(all_q, level, send_sem.at[0], q_sem)
         else:
             forward_level(all_q, level, send_sem.at[0], q_sem)
         forward_level(all_s, level, send_sem.at[1], s_sem)
@@ -292,10 +290,12 @@
         denominators.append(jnp.sum(expo, axis=1, keepdims=True) + self_expo)
         probs.append(expo.astype(BF16))
         selfs.append(self_expo.astype(BF16).astype(F32))
+    if levels:
+        forward_level(all_vr, 0, send_sem.at[2], vr_sem)
     for slot in range(rows):
         value_copies[slot].wait()
         mixed_ref[slot] = jnp.dot(probs[slot], values[slot], preferred_element_type=F32)
-    for level in range(levels):
+    for level in range(1, levels):
         forward_level(all_vr, level, send_sem.at[2], vr_sem)
 
     gains = gain[...]

time: 34.2 us -> 33.9 us (level)
    pallas_call x1, Pallas kernels: 32.6 us -> 32.3 us  [body(): pl.pallas_call(functools.partial(layer_kernel, (experts, beams, minor, ca...]
where the time goes in v3:
time: 33.9 us; the launch traced here: 33.6 us
  Pallas kernels  32.3 us (95%)
  local copies, waits for them, and re-layouts  1.33 us (4%)
    pallas_call x1, Pallas kernels, body(): pl.pallas_call(functools.partial(layer_kernel, (experts, beams, minor, ca...  32.3 us
    unnamed x1, local copies, waits for them, and re-layouts  1.33 us

profile of v3, /device:TPU:0, one launch (start us, length us, event | category | flops | bytes accessed | tf_op | source)
XLA Modules:
  0.0 33.6 jit_solution(10052256319458844249)
XLA Ops:
  0.0 32.3 %shard_map.127 = bf16[4,2048]{1,0:T(4,128)(2,1)} custom-call(s32[64]{0:T(128)} %parent_in.1, s32[6,64]{1,0:T(8,128)} %bitcast.4, f32[6,64]{1,0:T(8,128)} %bitcast.5, f32[1,2048]{1,0:T(1,128)} %bitcast.3, bf16[4,2048]{1,0:T(4,128)(2,1)} %queries.1, bf16[4,2048]{1,0:T(4,128)(2,1)} %new_keys.1, bf16[4,2048]{1,0:T(4,128)(2,1)} %new_values.1, ...), custom_call_target="tpu_custom_call" | custom-call | tf_op jit(solution)/shard_map/pallas_call | solution.py:429
  32.3 1.3 %copy.15 = bf16[4,2048]{1,0:T(4,128)(2,1)} copy(bf16[4,2048]{1,0:T(4,128)(2,1)} %shard_map.127) | data formatting | bytes 32768
